TPU v7x, 32 devices: a whole 2x2x4 slice. The times are simulated.
32 devices in a mesh: mem: 4 (over x, core), ty: 2 (over y), tx: 4 (over z).
Axes of the slice: x: 2, y: 2, z: 4, core: 2. Of those that a mesh axis runs over, the one named last changes fastest.
Arguments:
- pressure: float32 [8, 50, 64, 512], P('mem', None, 'ty', 'tx'), may hold values from -6 to 6
- east_wind: float32 [8, 50, 64, 512], P('mem', None, 'ty', 'tx'), may hold values from -6 to 6
- north_wind: float32 [8, 50, 64, 512], P('mem', None, 'ty', 'tx'), may hold values from -6 to 6
- vertical_wind: float32 [8, 49, 64, 512], P('mem', None, 'ty', 'tx'), may hold values from -6 to 6
- sound_squared: float32 [50, 64, 512], P(None, 'ty', 'tx'), may hold values from 0.5 to 2
- thickness: float32 [50], replicated, may hold values from 0.05 to 0.5
- owner_map: int32 [8], replicated, may hold values from 0 to 7, each once
Outputs:
- analysis: float32 [2, 4, 6, 32, 128], P('ty', 'tx', None, 'mem')
Inputs may be any that keep to these rules, and one draw needn't show every extreme that they name: `owner_map`: every tile index appears exactly once.
All inputs are finite; a program needn't handle non-finite values.
Results may differ from a plain program's by a relative error of at most 0.0001.
Values sent between devices are 32-bit elements; how exact they have to be, the bound alone decides.
A program may use at most 128 MiB of HBM per device.

v0:
```python
import jax
import jax.numpy as jnp
from jax import lax
from jax.sharding import PartitionSpec as P

SUBSTEPS = 2


horiz_ratio = 0.35
vert_ratio = 1.5


def shifted(block, axis, distance):
    devices = range(lax.axis_size(axis))
    route = [((i - distance) % len(devices), i) for i in devices]
    return lax.ppermute(block, axis, route)


def column_solve(coeff, rhs_list):
    count = len(rhs_list)
    factors = []
    values = []
    pivot = 1.0 + coeff[1] + coeff[0]
    values.append(rhs_list[0] / pivot)
    factors.append(-coeff[1] / pivot)
    for position in range(1, count):
        pivot = (
            1.0 + coeff[position + 1] + coeff[position] + coeff[position] * factors[position - 1]
        )
        values.append((rhs_list[position] + coeff[position] * values[position - 1]) / pivot)
        factors.append(-coeff[position + 1] / pivot)
    solved = [values[count - 1]]
    for position in range(count - 2, -1, -1):
        solved.insert(0, values[position] - factors[position] * solved[0])
    return solved


def substep_run(pressure, east_wind, north_wind, vertical_wind, sound_squared, coeff):
    levels = pressure.shape[1]
    western = shifted(pressure[..., -1:], "tx", 1)
    pressure_west = jnp.concatenate([western, pressure[..., :-1]], axis=3)
    southern = shifted(pressure[..., -1:, :], "ty", 1)
    pressure_south = jnp.concatenate([southern, pressure[..., :-1, :]], axis=2)
    east_wind = east_wind - horiz_ratio * (pressure - pressure_west)
    north_wind = north_wind - horiz_ratio * (pressure - pressure_south)
    eastern = shifted(east_wind[..., :1], "tx", -1)
    east_next = jnp.concatenate([east_wind[..., 1:], eastern], axis=3)
    northern = shifted(north_wind[..., :1, :], "ty", -1)
    north_next = jnp.concatenate([north_wind[..., 1:, :], northern], axis=2)
    divergence = east_next - east_wind + (north_next - north_wind)
    partial_value = pressure - horiz_ratio * sound_squared * divergence
    rhs_list = [
        vertical_wind[:, level]
        - vert_ratio * (partial_value[:, level + 1] - partial_value[:, level])
        for level in range(levels - 1)
    ]
    vertical_wind = jnp.stack(column_solve(coeff, rhs_list), axis=1)
    zero_layer = jnp.zeros_like(partial_value[:, :1])
    padded = jnp.concatenate([zero_layer, vertical_wind, zero_layer], axis=1)
    pressure = partial_value - vert_ratio * sound_squared * (padded[:, 1:] - padded[:, :-1])
    return (pressure, east_wind, north_wind, vertical_wind)


def finish_stats(first_sum, second_sum, members):
    mean = first_sum / members
    variance = second_sum / (members - 1)
    return jnp.concatenate([mean, variance], axis=0)


def local(pressure, east_wind, north_wind, vertical_wind, sound_squared, thickness, owner_map):
    levels = pressure.shape[1]
    rows_tile = pressure.shape[2]
    cols_tile = pressure.shape[3]
    members = pressure.shape[0] * lax.axis_size("mem")
    quarter = rows_tile // lax.axis_size("mem")
    coeff_field = vert_ratio * vert_ratio * sound_squared
    coeff = [coeff_field[level] for level in range(levels)]
    for substep in range(SUBSTEPS):
        pressure, east_wind, north_wind, vertical_wind = substep_run(
            pressure, east_wind, north_wind, vertical_wind, sound_squared, coeff
        )
    mass = jnp.einsum("k,mkyx->myx", thickness, pressure, precision=lax.Precision.HIGHEST)
    east_total = jnp.einsum("k,mkyx->myx", thickness, east_wind, precision=lax.Precision.HIGHEST)
    north_total = jnp.einsum("k,mkyx->myx", thickness, north_wind, precision=lax.Precision.HIGHEST)
    integrals = jnp.stack([mass, east_total, north_total], axis=1)
    first_local = jnp.sum(integrals, axis=0)
    ensemble_total = lax.psum(first_local, "mem")
    ensemble_mean = ensemble_total / members
    second_local = jnp.sum((integrals - ensemble_mean) ** 2, axis=0)
    my_tile = lax.axis_index(("ty", "tx"))
    row_start = lax.axis_index("mem") * quarter
    first_sum, second_sum = lax.psum((first_local, second_local), "mem")
    stats = finish_stats(first_sum, second_sum, members)
    weights = (owner_map == my_tile).astype(jnp.float32)
    rows_mine = lax.dynamic_slice_in_dim(
        lax.all_gather(stats[None], ("ty", "tx"), axis=0, tiled=True), row_start, quarter, 2
    )
    result = jnp.einsum("t,tsyx->syx", weights, rows_mine, precision=lax.Precision.HIGHEST)
    return result.reshape(1, 1, 6, quarter, cols_tile)


def solution(mesh):
    placed = (
        P("mem", None, "ty", "tx"),
        P("mem", None, "ty", "tx"),
        P("mem", None, "ty", "tx"),
        P("mem", None, "ty", "tx"),
        P(None, "ty", "tx"),
        P(),
        P(),
    )
    return jax.shard_map(
        local,
        mesh=mesh,
        in_specs=placed,
        out_specs=P("ty", "tx", None, "mem", None),
        check_vma=False,
    )
```

profile of v0, /device:TPU:0, one launch (start us, length us, event | category | flops | bytes accessed | tf_op | source)
XLA Modules:
  0.0 218.5 jit_solution(2176977665702427386)
XLA Ops:
  0.0 1.9 slice.749
  1.9 1.7 copy.808
  3.7 3.1 %collective-permute-start = (f32[2,50,32,1]{1,2,3,0:T(8,128)}, f32[2,50,32,1]{1,2,3,0:T(8,128)S(1)}, u32[]{:S(2)}, u32[]{:S(2)}) collective-permute-start(f32[2,50,32,1]{1,2,3,0:T(8,128)} %copy.808), channel_id=1, source_target_pairs={{3,0},{0,1},{1,2},{2,3},{7,4},{4,5},{5,6},{6,7},{11,8},{8,9},{9,10... | collective-permute-start | bytes 38408 | tf_op jit(solution)/shard_map/ppermute | solution.py:16
  6.9 1.6 collective-permute-start.2
  8.4 2.5 %broadcast_multiply_fusion.1 = (f32[50,32,128]{2,1,0:T(8,128)}, f32[50,32,128]{2,1,0:T(8,128)}, f32[50,32,128]{2,1,0:T(8,128)S(1)}) fusion(f32[50,32,128]{2,1,0:T(8,128)} %param.11), kind=kLoop, calls=%fused_computation.231 | loop fusion | flops 614400 | bytes 3276800 | tf_op jit(solution)/shard_map/mul | solution.py:60
  11.6 1.0 multiply_add_fusion.3
  41.0 2.5 %copy.733 = f32[2,50,32,1]{3,2,0,1:T(8,128)} copy(f32[2,50,32,1]{1,2,3,0:T(8,128)S(1)} %collective-permute-done) | data formatting | bytes 25600 | tf_op jit(solution)/shard_map/ppermute | solution.py:16
  43.7 4.8 %fusion.7 = (f32[2,50,32,128]{3,2,0,1:T(8,128)S(1)}, f32[2,50,32,128]{3,2,0,1:T(8,128)}) fusion(f32[2,50,32,1]{3,2,0,1:T(8,128)} %copy.733, f32[2,50,32,128]{3,2,1,0:T(8,128)} %param.8, f32[2,50,32,128]{3,2,1,0:T(8,128)S(1)} %copy-done.1, f32[2,50,1,128]{3,2,0,1:T(1,128)} %collective-permute-done.2, f32[2,50,32,128]{3,2,1,0:T(8,128)} %param.9), kind=kLoop, calls=%fused_computation.8 | loop fusion | flops 3276800 | bytes 11532800 | tf_op jit(solution)/shard_map/sub | solution.py:44
  48.4 1.8 copy.736
  50.2 2.2 %collective-permute-start.1 = (f32[2,50,32,1]{1,2,3,0:T(8,128)}, f32[2,50,32,1]{1,2,3,0:T(8,128)}, u32[]{:S(2)}, u32[]{:S(2)}) collective-permute-start(f32[2,50,32,1]{1,2,3,0:T(8,128)} %copy.736), channel_id=1, source_target_pairs={{1,0},{2,1},{3,2},{0,3},{5,4},{6,5},{7,6},{4,7},{9,8},{10,9},{11,1... | collective-permute-start | bytes 38408 | tf_op jit(solution)/shard_map/ppermute | solution.py:16
  52.4 1.6 slice.970
  55.0 1.6 slice.965
  56.6 1.6 slice.969
  58.2 3.3 %copy.737 = f32[2,50,32,1]{3,2,0,1:T(8,128)} copy(f32[2,50,32,1]{1,2,3,0:T(8,128)} %collective-permute-done.1) | data formatting | bytes 25600 | tf_op jit(solution)/shard_map/ppermute | solution.py:16
  61.8 4.7 %fusion.10 = f32[2,50,32,128]{3,2,0,1:T(8,128)S(1)} fusion(f32[2,50,32,128]{3,2,0,1:T(8,128)S(1)} %get-tuple-element.319, f32[2,50,32,1]{3,2,0,1:T(8,128)} %copy.737, f32[2,50,32,127]{3,2,0,1:T(8,128)} %slice.965, f32[2,50,32,128]{3,2,0,1:T(8,128)} %get-tuple-element.320, f32[2,50,1,128]{3,2,0,1:T(1,128)} %collective-permute-done.3, ...), kind=kLoop, calls=%fused_computation.12 | loop fusion | flops 2867200 | bytes 10649600 | tf_op jit(solution)/shard_map/sub | solution.py:51
  66.8 2.5 %add_divide_fusion.50 = (f32[2,1,32,128]{3,2,0,1:T(8,128)S(1)}, f32[2,1,32,128]{3,2,0,1:T(8,128)S(1)}, f32[2,1,32,128]{3,2,0,1:T(8,128)S(1)}, f32[2,1,32,128]{3,...) fusion(f32[32,128]{1,0:T(8,128)} %bitcast.1801, ...), kind=kLoop, calls=%fused_computation.760 | loop fusion | flops 1851392 | bytes 5619712 | tf_op jit(solution)/shard_map/div | solution.py:30
  69.7 3.2 %constant_dynamic-update-slice_fusion.98 = (f32[2,50,32,128]{3,2,0,1:T(8,128)S(1)}, f32[2,1,32,128]{3,2,0,1:T(8,128)}, f32[2,1,32,128]{3,2,0,1:T(8,128)}, f32[2,...) fusion(f32[2,50,32,128]{3,2,0,1:T(8,128)S(1)} %copy-done.8, ...), kind=kLoop, calls=%fused_computation.128 | loop fusion | flops 1777664 | bytes 5554176
  72.9 0.8 constant_dynamic-update-slice_fusion.49
  73.7 0.8 constant_dynamic-update-slice_fusion.97
  74.5 0.8 constant_dynamic-update-slice_fusion.96
  75.3 0.8 constant_dynamic-update-slice_fusion.95
  79.1 0.8 constant_dynamic-update-slice_fusion.90
  81.7 0.8 constant_dynamic-update-slice_fusion.87
  106.1 1.7 fusion.149
  107.9 1.0 constant_dynamic-update-slice_fusion.56
  111.4 1.8 copy.792
  113.1 1.7 collective-permute-start.6
  115.5 3.6 %collective-permute-done.4 = f32[2,50,32,1]{1,2,3,0:T(8,128)S(1)} collective-permute-done((f32[2,50,32,1]{1,2,3,0:T(8,128)}, f32[2,50,32,1]{1,2,3,0:T(8,128)S(1)}, u32[]{:S(2)}, u32[]{:S(2)}) %collective-permute-start.4) | collective-permute-done | bytes 12832 | tf_op jit(solution)/shard_map/ppermute | solution.py:16
  119.0 2.6 %copy.793 = f32[2,50,32,1]{3,2,0,1:T(8,128)} copy(f32[2,50,32,1]{1,2,3,0:T(8,128)S(1)} %collective-permute-done.4) | data formatting | bytes 25600 | tf_op jit(solution)/shard_map/ppermute | solution.py:16
  122.2 4.8 %fusion.14 = (f32[2,50,32,128]{3,2,0,1:T(8,128)S(1)}, f32[2,50,32,128]{3,2,0,1:T(8,128)}) fusion(f32[2,50,32,128]{3,2,0,1:T(8,128)} %copy-done.2, f32[2,50,32,128]{3,2,0,1:T(8,128)S(1)} %multiply_subtract_fusion.1, f32[2,50,32,127]{3,2,0,1:T(8,128)S(1)} %bitcast.1630, f32[2,50,32,1]{3,2,0,1:T(8,128)} %copy.793, f32[2,50,32,128]{3,2,0,1:T(8,128)} %get-tuple-element.320, ...), kind=kLoop, calls=%fused_computation.19 | loop fusion | flops 3276800 | bytes 11468800 | tf_op jit(solution)/shard_map/sub | solution.py:44
  127.0 1.8 copy.794
  129.0 1.8 slice.1078
  130.8 1.5 collective-permute-start.7
  132.3 2.7 %fusion.2 = f32[1,2,32,128]{3,0,2,1:T(1,128)} fusion(f32[2,50,32,128]{3,2,0,1:T(8,128)S(1)} %get-tuple-element.317, f32[50]{0:T(128)S(1)} %copy-done), kind=kOutput, calls=%fused_computation.2 | convolution fusion | flops 4915200 | bytes 1671368 | tf_op jit(solution)/shard_map/k,mkyx->myx/dot_general | solution.py:83
  135.0 2.7 %fusion = f32[1,2,32,128]{3,0,2,1:T(1,128)} fusion(f32[2,50,32,128]{3,2,0,1:T(8,128)S(1)} %copy-done.3, f32[50]{0:T(128)S(1)} %copy-done), kind=kOutput, calls=%fused_computation | convolution fusion | flops 4915200 | bytes 1671368 | tf_op jit(solution)/shard_map/k,mkyx->myx/dot_general | solution.py:84
  137.7 1.7 slice.1073
  139.4 1.5 slice.1077
  140.9 3.3 %copy.795 = f32[2,50,32,1]{3,2,0,1:T(8,128)} copy(f32[2,50,32,1]{1,2,3,0:T(8,128)} %collective-permute-done.5) | data formatting | bytes 25600 | tf_op jit(solution)/shard_map/ppermute | solution.py:16
  144.6 4.6 %fusion.17 = f32[2,50,32,128]{3,2,0,1:T(8,128)S(1)} fusion(f32[2,50,32,128]{3,2,0,1:T(8,128)S(1)} %multiply_subtract_fusion.1, f32[2,50,32,128]{3,2,0,1:T(8,128)S(1)} %get-tuple-element.317, f32[2,50,32,1]{3,2,0,1:T(8,128)} %copy.795, f32[2,50,32,127]{3,2,0,1:T(8,128)} %slice.1073, f32[2,50,32,128]{3,2,0,1:T(8,128)} %get-tuple-element.318, ...), kind=kLoop, calls=%fused_computation.23 | loop fusion | flops 2867200 | bytes 10649600 | tf_op jit(solution)/shard_map/sub | solution.py:51
  149.6 3.4 %fusion.32 = (f32[2,32,128]{2,1,0:T(8,128)S(1)}, f32[2,32,128]{2,1,0:T(8,128)S(1)}, f32[2,32,128]{2,1,0:T(8,128)S(1)}, f32[2,32,128]{2,1,0:T(8,128)S(1)}, f32[2,...) fusion(f32[2,32,128]{2,1,0:T(8,128)} %copy-done.207, f32[32,128]{1,0:T(8,128)} %get-tuple-element.258, ...), kind=kLoop, calls=%fused_computation.301 | loop fusion | flops 4046848 | bytes 5652480 | tf_op jit(solution)/shard_map/div | solution.py:30
  153.0 2.4 %add_divide_fusion = (f32[2,1,32,128]{3,2,0,1:T(8,128)S(1)}, f32[2,1,32,128]{3,2,0,1:T(8,128)S(1)}, f32[2,1,32,128]{3,2,0,1:T(8,128)S(1)}, f32[2,1,32,128]{3,2,0...) fusion(f32[2,1,32,128]{3,2,0,1:T(8,128)} %get-tuple-element.149, ...), kind=kLoop, calls=%fused_computation.616 | loop fusion | flops 1949696 | bytes 5259264 | tf_op jit(solution)/shard_map/div | solution.py:30
  155.4 2.2 %constant_dynamic-update-slice_fusion.198 = (f32[2,50,32,128]{3,2,0,1:T(8,128)S(1)}, f32[2,1,32,128]{3,2,0,1:T(8,128)S(1)}, f32[2,1,32,128]{3,2,0,1:T(8,128)S(1)...) fusion(f32[2,50,32,128]{3,2,0,1:T(8,128)S(1)} %copy-done.7, ...), kind=kLoop, calls=%fused_computation.228 | loop fusion | flops 1548288 | bytes 4456448
  159.3 0.8 multiply_subtract_fusion
  160.1 2.3 %fusion.4 = f32[1,2,32,128]{3,0,2,1:T(1,128)S(1)} fusion(f32[2,50,32,128]{3,2,0,1:T(8,128)S(1)} %multiply_subtract_fusion, f32[50]{0:T(128)S(1)} %copy-done), kind=kOutput, calls=%fused_computation.4 | convolution fusion | flops 4915200 | bytes 1671368 | tf_op jit(solution)/shard_map/k,mkyx->myx/dot_general | solution.py:82
  162.5 10.5 %psum.14 = f32[3,32,128]{2,1,0:T(8,128)S(1)} all-reduce(f32[3,32,128]{2,1,0:T(8,128)S(1)} %fusion.22), channel_id=1, replica_groups=mesh['mem'=4,'ty'=2,'tx'=4] {'mem'}, use_global_device_ids=true, to_apply=%region_1.0 | all-reduce | flops 12288 | bytes 98304 | tf_op jit(solution)/shard_map/psum | solution.py:92
  173.0 11.2 %psum.18 = f32[3,32,128]{2,1,0:T(8,128)S(1)} all-reduce(f32[3,32,128]{2,1,0:T(8,128)S(1)} %multiply_reduce_fusion), channel_id=1, replica_groups=mesh['mem'=4,'ty'=2,'tx'=4] {'mem'}, use_global_device_ids=true, to_apply=%region_3.0 | all-reduce | flops 12288 | bytes 98304 | tf_op jit(solution)/shard_map/psum | solution.py:92
  184.3 33.3 %all-gather = f32[48,32,128]{2,1,0:T(8,128)S(1)} all-gather(f32[6,32,128]{2,1,0:T(8,128)S(1)} %pad_maximum_fusion.1), channel_id=2, replica_groups=mesh['mem'=4,'ty'=2,'tx'=4] {'ty','tx'}, dimensions={0}, use_global_device_ids=true | all-gather | bytes 884736 | tf_op jit(solution)/shard_map/all_gather | solution.py:96
  217.6 0.9 fusion.20
  (594 shorter events, 63.2 us)
Async XLA Ops:
  0.0 132.3 %copy-start = (f32[50]{0:T(128)S(1)}, f32[50]{0:T(128)}, u32[]{:S(2)}) copy-start(f32[50]{0:T(128)} %param.12) | copy-start | bytes 604
  3.7 37.3 %collective-permute-start = (f32[2,50,32,1]{1,2,3,0:T(8,128)}, f32[2,50,32,1]{1,2,3,0:T(8,128)S(1)}, u32[]{:S(2)}, u32[]{:S(2)}) collective-permute-start(f32[2,50,32,1]{1,2,3,0:T(8,128)} %copy.808), channel_id=1, source_target_pairs={{3,0},{0,1},{1,2},{2,3},{7,4},{4,5},{5,6},{6,7},{11,8},{8,9},{9,10... | collective-permute-start | bytes 38408 | tf_op jit(solution)/shard_map/ppermute | solution.py:16
  6.9 36.8 %collective-permute-start.2 = (f32[2,50,1,128]{3,2,0,1:T(1,128)S(1)}, f32[2,50,1,128]{3,2,0,1:T(1,128)}, u32[]{:S(2)}, u32[]{:S(2)}) collective-permute-start(f32[2,50,1,128]{3,2,0,1:T(1,128)S(1)} %copy.872), channel_id=1, source_target_pairs={{4,0},{0,4},{5,1},{1,5},{6,2},{2,6},{7,3},{3,7},{12,8},{8,12},{13,... | collective-permute-start | bytes 153608 | tf_op jit(solution)/shard_map/ppermute | solution.py:16
  50.2 8.0 %collective-permute-start.1 = (f32[2,50,32,1]{1,2,3,0:T(8,128)}, f32[2,50,32,1]{1,2,3,0:T(8,128)}, u32[]{:S(2)}, u32[]{:S(2)}) collective-permute-start(f32[2,50,32,1]{1,2,3,0:T(8,128)} %copy.736), channel_id=1, source_target_pairs={{1,0},{2,1},{3,2},{0,3},{5,4},{6,5},{7,6},{4,7},{9,8},{10,9},{11,1... | collective-permute-start | bytes 38408 | tf_op jit(solution)/shard_map/ppermute | solution.py:16
  54.1 7.4 %collective-permute-start.3 = (f32[2,50,1,128]{3,2,0,1:T(1,128)}, f32[2,50,1,128]{3,2,0,1:T(1,128)}, u32[]{:S(2)}, u32[]{:S(2)}) collective-permute-start(f32[2,50,1,128]{3,2,0,1:T(1,128)} %slice.970), channel_id=1, source_target_pairs={{4,0},{0,4},{5,1},{1,5},{6,2},{2,6},{7,3},{3,7},{12,8},{8,12},{13,... | collective-permute-start | bytes 153608 | tf_op jit(solution)/shard_map/ppermute | solution.py:16
  69.3 36.1 %copy-start.138 = (f32[2,1,32,128]{3,2,0,1:T(8,128)}, f32[2,1,32,128]{3,2,0,1:T(8,128)S(1)}, u32[]{:S(2)}) copy-start(f32[2,1,32,128]{3,2,0,1:T(8,128)S(1)} %get-tuple-element.261) | copy-start | bytes 98308
  69.3 36.1 %copy-start.139 = (f32[2,1,32,128]{3,2,0,1:T(8,128)}, f32[2,1,32,128]{3,2,0,1:T(8,128)S(1)}, u32[]{:S(2)}) copy-start(f32[2,1,32,128]{3,2,0,1:T(8,128)S(1)} %get-tuple-element.264) | copy-start | bytes 98308
  69.3 36.1 %copy-start.140 = (f32[2,1,32,128]{3,2,0,1:T(8,128)}, f32[2,1,32,128]{3,2,0,1:T(8,128)S(1)}, u32[]{:S(2)}) copy-start(f32[2,1,32,128]{3,2,0,1:T(8,128)S(1)} %get-tuple-element.267) | copy-start | bytes 98308
  69.3 36.1 %copy-start.141 = (f32[2,1,32,128]{3,2,0,1:T(8,128)}, f32[2,1,32,128]{3,2,0,1:T(8,128)S(1)}, u32[]{:S(2)}) copy-start(f32[2,1,32,128]{3,2,0,1:T(8,128)S(1)} %get-tuple-element.270) | copy-start | bytes 98308
  69.3 36.1 %copy-start.142 = (f32[2,1,32,128]{3,2,0,1:T(8,128)}, f32[2,1,32,128]{3,2,0,1:T(8,128)S(1)}, u32[]{:S(2)}) copy-start(f32[2,1,32,128]{3,2,0,1:T(8,128)S(1)} %get-tuple-element.273) | copy-start | bytes 98308
  69.4 36.1 %copy-start.143 = (f32[2,1,32,128]{3,2,0,1:T(8,128)}, f32[2,1,32,128]{3,2,0,1:T(8,128)S(1)}, u32[]{:S(2)}) copy-start(f32[2,1,32,128]{3,2,0,1:T(8,128)S(1)} %get-tuple-element.276) | copy-start | bytes 98308
  69.4 36.1 %copy-start.144 = (f32[2,1,32,128]{3,2,0,1:T(8,128)}, f32[2,1,32,128]{3,2,0,1:T(8,128)S(1)}, u32[]{:S(2)}) copy-start(f32[2,1,32,128]{3,2,0,1:T(8,128)S(1)} %get-tuple-element.279) | copy-start | bytes 98308
  69.4 36.1 %copy-start.145 = (f32[2,1,32,128]{3,2,0,1:T(8,128)}, f32[2,1,32,128]{3,2,0,1:T(8,128)S(1)}, u32[]{:S(2)}) copy-start(f32[2,1,32,128]{3,2,0,1:T(8,128)S(1)} %get-tuple-element.282) | copy-start | bytes 98308
  69.4 36.1 %copy-start.146 = (f32[2,1,32,128]{3,2,0,1:T(8,128)}, f32[2,1,32,128]{3,2,0,1:T(8,128)S(1)}, u32[]{:S(2)}) copy-start(f32[2,1,32,128]{3,2,0,1:T(8,128)S(1)} %get-tuple-element.285) | copy-start | bytes 98308
  69.4 36.1 %copy-start.147 = (f32[2,1,32,128]{3,2,0,1:T(8,128)}, f32[2,1,32,128]{3,2,0,1:T(8,128)S(1)}, u32[]{:S(2)}) copy-start(f32[2,1,32,128]{3,2,0,1:T(8,128)S(1)} %get-tuple-element.288) | copy-start | bytes 98308
  69.4 36.1 %copy-start.148 = (f32[2,1,32,128]{3,2,0,1:T(8,128)}, f32[2,1,32,128]{3,2,0,1:T(8,128)S(1)}, u32[]{:S(2)}) copy-start(f32[2,1,32,128]{3,2,0,1:T(8,128)S(1)} %get-tuple-element.291) | copy-start | bytes 98308
  69.4 36.1 %copy-start.149 = (f32[2,1,32,128]{3,2,0,1:T(8,128)}, f32[2,1,32,128]{3,2,0,1:T(8,128)S(1)}, u32[]{:S(2)}) copy-start(f32[2,1,32,128]{3,2,0,1:T(8,128)S(1)} %get-tuple-element.294) | copy-start | bytes 98308
  69.4 36.1 %copy-start.150 = (f32[2,1,32,128]{3,2,0,1:T(8,128)}, f32[2,1,32,128]{3,2,0,1:T(8,128)S(1)}, u32[]{:S(2)}) copy-start(f32[2,1,32,128]{3,2,0,1:T(8,128)S(1)} %get-tuple-element.297) | copy-start | bytes 98308
  69.4 36.1 %copy-start.151 = (f32[2,1,32,128]{3,2,0,1:T(8,128)}, f32[2,1,32,128]{3,2,0,1:T(8,128)S(1)}, u32[]{:S(2)}) copy-start(f32[2,1,32,128]{3,2,0,1:T(8,128)S(1)} %get-tuple-element.300) | copy-start | bytes 98308
  69.4 36.1 %copy-start.152 = (f32[2,1,32,128]{3,2,0,1:T(8,128)}, f32[2,1,32,128]{3,2,0,1:T(8,128)S(1)}, u32[]{:S(2)}) copy-start(f32[2,1,32,128]{3,2,0,1:T(8,128)S(1)} %get-tuple-element.303) | copy-start | bytes 98308
  69.5 36.1 %copy-start.153 = (f32[2,1,32,128]{3,2,0,1:T(8,128)}, f32[2,1,32,128]{3,2,0,1:T(8,128)S(1)}, u32[]{:S(2)}) copy-start(f32[2,1,32,128]{3,2,0,1:T(8,128)S(1)} %get-tuple-element.306) | copy-start | bytes 98308
  69.5 36.1 %copy-start.154 = (f32[2,1,32,128]{3,2,0,1:T(8,128)}, f32[2,1,32,128]{3,2,0,1:T(8,128)S(1)}, u32[]{:S(2)}) copy-start(f32[2,1,32,128]{3,2,0,1:T(8,128)S(1)} %get-tuple-element.309) | copy-start | bytes 98308
  69.5 36.1 %copy-start.155 = (f32[2,1,32,128]{3,2,0,1:T(8,128)}, f32[2,1,32,128]{3,2,0,1:T(8,128)S(1)}, u32[]{:S(2)}) copy-start(f32[2,1,32,128]{3,2,0,1:T(8,128)S(1)} %get-tuple-element.312) | copy-start | bytes 98308
  69.5 36.1 %copy-start.156 = (f32[2,1,32,128]{3,2,0,1:T(8,128)}, f32[2,1,32,128]{3,2,0,1:T(8,128)S(1)}, u32[]{:S(2)}) copy-start(f32[2,1,32,128]{3,2,0,1:T(8,128)S(1)} %get-tuple-element.315) | copy-start | bytes 98308
  69.5 36.1 %copy-start.190 = (f32[2,1,32,128]{3,2,0,1:T(8,128)}, f32[2,1,32,128]{3,2,0,1:T(8,128)S(1)}, u32[]{:S(2)}) copy-start(f32[2,1,32,128]{3,2,0,1:T(8,128)S(1)} %get-tuple-element.262) | copy-start | bytes 98308
  69.5 36.1 %copy-start.191 = (f32[2,1,32,128]{3,2,0,1:T(8,128)}, f32[2,1,32,128]{3,2,0,1:T(8,128)S(1)}, u32[]{:S(2)}) copy-start(f32[2,1,32,128]{3,2,0,1:T(8,128)S(1)} %get-tuple-element.265) | copy-start | bytes 98308
  69.5 36.1 %copy-start.192 = (f32[2,1,32,128]{3,2,0,1:T(8,128)}, f32[2,1,32,128]{3,2,0,1:T(8,128)S(1)}, u32[]{:S(2)}) copy-start(f32[2,1,32,128]{3,2,0,1:T(8,128)S(1)} %get-tuple-element.268) | copy-start | bytes 98308
  69.5 36.1 %copy-start.193 = (f32[2,1,32,128]{3,2,0,1:T(8,128)}, f32[2,1,32,128]{3,2,0,1:T(8,128)S(1)}, u32[]{:S(2)}) copy-start(f32[2,1,32,128]{3,2,0,1:T(8,128)S(1)} %get-tuple-element.271) | copy-start | bytes 98308
  69.5 36.1 %copy-start.194 = (f32[2,1,32,128]{3,2,0,1:T(8,128)}, f32[2,1,32,128]{3,2,0,1:T(8,128)S(1)}, u32[]{:S(2)}) copy-start(f32[2,1,32,128]{3,2,0,1:T(8,128)S(1)} %get-tuple-element.274) | copy-start | bytes 98308
  69.5 36.1 %copy-start.195 = (f32[2,1,32,128]{3,2,0,1:T(8,128)}, f32[2,1,32,128]{3,2,0,1:T(8,128)S(1)}, u32[]{:S(2)}) copy-start(f32[2,1,32,128]{3,2,0,1:T(8,128)S(1)} %get-tuple-element.277) | copy-start | bytes 98308
  69.6 36.1 %copy-start.196 = (f32[2,1,32,128]{3,2,0,1:T(8,128)}, f32[2,1,32,128]{3,2,0,1:T(8,128)S(1)}, u32[]{:S(2)}) copy-start(f32[2,1,32,128]{3,2,0,1:T(8,128)S(1)} %get-tuple-element.280) | copy-start | bytes 98308
  69.6 36.1 %copy-start.197 = (f32[2,1,32,128]{3,2,0,1:T(8,128)}, f32[2,1,32,128]{3,2,0,1:T(8,128)S(1)}, u32[]{:S(2)}) copy-start(f32[2,1,32,128]{3,2,0,1:T(8,128)S(1)} %get-tuple-element.283) | copy-start | bytes 98308
  69.6 36.1 %copy-start.198 = (f32[2,1,32,128]{3,2,0,1:T(8,128)}, f32[2,1,32,128]{3,2,0,1:T(8,128)S(1)}, u32[]{:S(2)}) copy-start(f32[2,1,32,128]{3,2,0,1:T(8,128)S(1)} %get-tuple-element.286) | copy-start | bytes 98308
  69.6 36.1 %copy-start.199 = (f32[2,1,32,128]{3,2,0,1:T(8,128)}, f32[2,1,32,128]{3,2,0,1:T(8,128)S(1)}, u32[]{:S(2)}) copy-start(f32[2,1,32,128]{3,2,0,1:T(8,128)S(1)} %get-tuple-element.289) | copy-start | bytes 98308
  69.6 36.1 %copy-start.200 = (f32[2,1,32,128]{3,2,0,1:T(8,128)}, f32[2,1,32,128]{3,2,0,1:T(8,128)S(1)}, u32[]{:S(2)}) copy-start(f32[2,1,32,128]{3,2,0,1:T(8,128)S(1)} %get-tuple-element.292) | copy-start | bytes 98308
  69.6 36.1 %copy-start.201 = (f32[2,1,32,128]{3,2,0,1:T(8,128)}, f32[2,1,32,128]{3,2,0,1:T(8,128)S(1)}, u32[]{:S(2)}) copy-start(f32[2,1,32,128]{3,2,0,1:T(8,128)S(1)} %get-tuple-element.295) | copy-start | bytes 98308
  69.6 36.1 %copy-start.202 = (f32[2,1,32,128]{3,2,0,1:T(8,128)}, f32[2,1,32,128]{3,2,0,1:T(8,128)S(1)}, u32[]{:S(2)}) copy-start(f32[2,1,32,128]{3,2,0,1:T(8,128)S(1)} %get-tuple-element.298) | copy-start | bytes 98308
  72.9 32.9 %copy-start.136 = (f32[2,1,32,128]{3,2,0,1:T(8,128)}, f32[2,1,32,128]{3,2,0,1:T(8,128)S(1)}, u32[]{:S(2)}) copy-start(f32[2,1,32,128]{3,2,0,1:T(8,128)S(1)} %get-tuple-element.152) | copy-start | bytes 98308
  72.9 32.9 %copy-start.137 = (f32[2,1,32,128]{3,2,0,1:T(8,128)}, f32[2,1,32,128]{3,2,0,1:T(8,128)S(1)}, u32[]{:S(2)}) copy-start(f32[2,1,32,128]{3,2,0,1:T(8,128)S(1)} %get-tuple-element.153) | copy-start | bytes 98308
  72.9 32.9 %copy-start.187 = (f32[2,1,32,128]{3,2,0,1:T(8,128)}, f32[2,1,32,128]{3,2,0,1:T(8,128)S(1)}, u32[]{:S(2)}) copy-start(f32[2,1,32,128]{3,2,0,1:T(8,128)S(1)} %get-tuple-element.154) | copy-start | bytes 98308
  72.9 32.9 %copy-start.188 = (f32[2,1,32,128]{3,2,0,1:T(8,128)}, f32[2,1,32,128]{3,2,0,1:T(8,128)S(1)}, u32[]{:S(2)}) copy-start(f32[2,1,32,128]{3,2,0,1:T(8,128)S(1)} %get-tuple-element.156) | copy-start | bytes 98308
  72.9 34.9 %copy-start.157 = (f32[2,1,32,128]{3,2,0,1:T(8,128)}, f32[2,1,32,128]{3,2,0,1:T(8,128)S(1)}, u32[]{:S(2)}) copy-start(f32[2,1,32,128]{3,2,0,1:T(8,128)S(1)} %get-tuple-element.155) | copy-start | bytes 98308
  72.9 34.9 %copy-start.158 = (f32[2,1,32,128]{3,2,0,1:T(8,128)}, f32[2,1,32,128]{3,2,0,1:T(8,128)S(1)}, u32[]{:S(2)}) copy-start(f32[2,1,32,128]{3,2,0,1:T(8,128)S(1)} %get-tuple-element.157) | copy-start | bytes 98308
  113.1 5.9 %collective-permute-start.4 = (f32[2,50,32,1]{1,2,3,0:T(8,128)}, f32[2,50,32,1]{1,2,3,0:T(8,128)S(1)}, u32[]{:S(2)}, u32[]{:S(2)}) collective-permute-start(f32[2,50,32,1]{1,2,3,0:T(8,128)} %copy.792), channel_id=1, source_target_pairs={{3,0},{0,1},{1,2},{2,3},{7,4},{4,5},{5,6},{6,7},{11,8},{8,9},{9,10... | collective-permute-start | bytes 38408 | tf_op jit(solution)/shard_map/ppermute | solution.py:16
  113.1 8.5 %collective-permute-start.6 = (f32[2,50,1,128]{3,2,0,1:T(1,128)}, f32[2,50,1,128]{3,2,0,1:T(1,128)S(1)}, u32[]{:S(2)}, u32[]{:S(2)}) collective-permute-start(f32[2,50,1,128]{3,2,0,1:T(1,128)} %slice.1075), channel_id=1, source_target_pairs={{4,0},{0,4},{5,1},{1,5},{6,2},{2,6},{7,3},{3,7},{12,8},{8,12},{13,... | collective-permute-start | bytes 153608 | tf_op jit(solution)/shard_map/ppermute | solution.py:16
  128.8 12.1 %collective-permute-start.5 = (f32[2,50,32,1]{1,2,3,0:T(8,128)}, f32[2,50,32,1]{1,2,3,0:T(8,128)}, u32[]{:S(2)}, u32[]{:S(2)}) collective-permute-start(f32[2,50,32,1]{1,2,3,0:T(8,128)} %copy.794), channel_id=1, source_target_pairs={{1,0},{2,1},{3,2},{0,3},{5,4},{6,5},{7,6},{4,7},{9,8},{10,9},{11,1... | collective-permute-start | bytes 38408 | tf_op jit(solution)/shard_map/ppermute | solution.py:16
  130.8 13.8 %collective-permute-start.7 = (f32[2,50,1,128]{3,2,0,1:T(1,128)}, f32[2,50,1,128]{3,2,0,1:T(1,128)}, u32[]{:S(2)}, u32[]{:S(2)}) collective-permute-start(f32[2,50,1,128]{3,2,0,1:T(1,128)} %slice.1078), channel_id=1, source_target_pairs={{4,0},{0,4},{5,1},{1,5},{6,2},{2,6},{7,3},{3,7},{12,8},{8,12},{13,... | collective-permute-start | bytes 153608 | tf_op jit(solution)/shard_map/ppermute | solution.py:16
  160.1 57.5 %copy-start.214 = (s32[8]{0:T(128)S(1)}, s32[8]{0:T(128)}, u32[]{:S(2)}) copy-start(s32[8]{0:T(128)} %param.13) | copy-start | bytes 100
  (175 other events, 1667.4 us)
where the time goes:
time: 222 us; the launch traced here: 219 us
  other arithmetic  69 us (31%)
  local copies, waits for them, and re-layouts  68.2 us (31%)
  blocking collectives  55 us (25%)
  starting transfers between devices  10.6 us (5%)
  matrix products  8.58 us (4%)
  waiting for transfers between devices  3.6 us (2%)
  between operations  3.49 us (2%)
    unnamed x528, local copies, waits for them, and re-layouts  38.2 us
    all_gather x1, blocking collectives, local(): lax.all_gather(stats[None], ('ty', 'tx'), axis=0, tiled=True)  33.3 us
    mul x42, other arithmetic, column_solve(): solved.insert(0, values[position] - factors[position] * solved[0])  26.3 us
    psum x2, blocking collectives, local(): first_sum, second_sum = lax.psum((first_local, second_local), 'mem')  21.7 us
    ppermute x4, local copies, waits for them, and re-layouts, shifted(): return lax.ppermute(block, axis, route)  11.6 us
    ppermute x8, starting transfers between devices, shifted(): return lax.ppermute(block, axis, route)  10.6 us
    div x4, other arithmetic, column_solve(): (rhs_list[position] + coeff[position] * values[position - 1]) / pivot  9.91 us
    sub x2, other arithmetic, substep_run(): east_wind = east_wind - horiz_ratio * (pressure - pressure_west)  9.56 us
  transfers between devices with their start and end apart: 8, of which 1 were waited for; matrix products, arithmetic and copies ran while one was open for 28% of the time, Pallas kernels for 0%

commit v1 on v0

v1 whole, which is shorter than its diff:
```python
import functools

import jax
import jax.numpy as jnp
from jax import lax
from jax.experimental import pallas as pl
from jax.experimental.pallas import tpu as pltpu
from jax.sharding import PartitionSpec as P

SUBSTEPS = 2
MESH = pl.DeviceIdType.MESH

horiz_ratio = 0.35
vert_ratio = 1.5


def unrolled(count, body, carry, most=7):
    width = max(d for d in range(1, most + 1) if count % d == 0)

    def block(i, c):
        for j in range(width):
            c = body(i * width + j, c)
        return c

    return lax.fori_loop(0, count // width, block, carry)


def kernel(
    sizes,
    p_hbm, u_hbm, v_hbm, w_hbm, s_hbm, thick, owner,
    out,
    p, u, v, w, s, inv, g,
    csend, crecv, rsend, rrecv, ueast, vnorth,
    integ, gath, everyone,
    load_sem, cs_sem, cr_sem, rs_sem, rr_sem, ms_sem, mr_sem, as_sem, ar_sem,
):
    n_mem, n_ty, n_tx = sizes
    own, levels, rows, cols = p.shape
    quarter = rows // n_mem
    tiles = n_ty * n_tx
    mem, ty, tx = lax.axis_index("mem"), lax.axis_index("ty"), lax.axis_index("tx")
    me = ty * n_tx + tx
    east, west = {"tx": lax.rem(tx + 1, n_tx)}, {"tx": lax.rem(tx + n_tx - 1, n_tx)}
    north, south = {"ty": lax.rem(ty + 1, n_ty)}, {"ty": lax.rem(ty + n_ty - 1, n_ty)}
    lane = lax.broadcasted_iota(jnp.int32, (rows, cols), 1)
    row = lax.broadcasted_iota(jnp.int32, (rows, cols), 0)
    zero = jnp.zeros((rows, cols), jnp.float32)

    def load(src, dst, sem):
        copy = pltpu.make_async_copy(src, dst, load_sem.at[sem])
        copy.start()
        return copy

    loads = {}
    for m in range(own):
        for i, (name, src, dst) in enumerate((("p", p_hbm, p), ("u", u_hbm, u), ("v", v_hbm, v))):
            loads[name, m] = load(src.at[m], dst.at[m], 4 * m + i)
        if m == 0:
            loads["s"] = load(s_hbm, s, 4 * own)
    for m in range(own):
        loads["w", m] = load(w_hbm.at[m], w.at[m], 4 * m + 3)

    barrier = pltpu.get_barrier_semaphore()

    def tile_id(i):
        other = lax.rem(me + i, tiles)
        return other, {"ty": lax.div(other, n_tx), "tx": lax.rem(other, n_tx)}

    def mem_id(i):
        other = lax.rem(mem + i, n_mem)
        return other, {"mem": other}

    for i in range(1, tiles):
        pl.semaphore_signal(barrier, inc=1, device_id=tile_id(i)[1], device_id_type=MESH)
    for i in range(1, n_mem):
        pl.semaphore_signal(barrier, inc=1, device_id=mem_id(i)[1], device_id_type=MESH)

    def remote(src, dst, ssem, rsem, where):
        return pltpu.make_async_remote_copy(
            src_ref=src, dst_ref=dst, send_sem=ssem, recv_sem=rsem, device_id=where, device_id_type=MESH
        )

    def halo_copies(sub, m):
        kinds = ((0, east, north), (1, west, south), (2, west, south))
        copies = []
        for kind, across, along in kinds if sub == 0 else kinds[:2]:
            copies.append(remote(
                rsend.at[sub, m, kind], rrecv.at[sub, m, kind],
                rs_sem.at[sub, m, kind], rr_sem.at[sub, m, kind], along))
            copies.append(remote(
                csend.at[sub, m, kind], crecv.at[sub, m, kind],
                cs_sem.at[sub, m, kind], cr_sem.at[sub, m, kind], across))
        return copies

    def pack_first(k, x, packed):
        return jnp.where(lane == cols - 1 - k, pltpu.roll(x, cols - 1 - k, 1), packed)

    def pack_last(k, x, packed):
        shift = cols - k if not isinstance(k, int) or k > 0 else 0
        return jnp.where(lane == cols - 1 - k, pltpu.roll(x, shift, 1), packed)

    def pack_inputs(m):
        def one(k, c):
            last, first, ufirst = c
            pk = p[m, k]
            first = pack_first(k, pk, first)
            last = jnp.where(lane == cols - 1 - k, pltpu.roll(pk, lax.rem(cols - k, cols), 1), last)
            ufirst = pack_first(k, u[m, k], ufirst)
            rsend[0, m, 0, pl.ds(k, 1), :] = p[m, k, rows - 1 : rows, :]
            rsend[0, m, 1, pl.ds(k, 1), :] = p[m, k, 0:1, :]
            rsend[0, m, 2, pl.ds(k, 1), :] = v[m, k, 0:1, :]
            return last, first, ufirst

        packs = unrolled(levels, one, (zero, zero, zero), 5)
        for kind in range(3):
            csend[0, m, kind] = packs[kind]

    def pivots():
        def one(i, c):
            k = i + 1
            below, gprev = c
            b = (vert_ratio * vert_ratio) * s[k]
            r = 1.0 / (1.0 + b + below - below * gprev)
            inv[k] = r
            gk = b * r
            g[k] = gk
            return b, gk

        unrolled(levels - 1, one, ((vert_ratio * vert_ratio) * s[0], zero))

    def forward(sub, m):
        last_sub = sub == SUBSTEPS - 1
        before = crecv[0, m, 2] if sub == 0 else ueast[m]
        ueast[m] = before - horiz_ratio * (crecv[sub, m, 1] - csend[sub, m, 0])
        before = rrecv[0, m, 2] if sub == 0 else vnorth[m]
        vnorth[m] = before - horiz_ratio * (rrecv[sub, m, 1] - rsend[sub, m, 0])

        def level(k):
            pk = p[m, k]
            pw = jnp.where(lane == 0, pltpu.roll(crecv[sub, m, 0], k + 1, 1), pltpu.roll(pk, 1, 1))
            ps = jnp.where(row == 0, rrecv[sub, m, 0, pl.ds(k, 1), :], pltpu.roll(pk, 1, 0))
            uk = u[m, k] - horiz_ratio * (pk - pw)
            vk = v[m, k] - horiz_ratio * (pk - ps)
            ue = jnp.where(lane == cols - 1, pltpu.roll(ueast[m], k, 1), pltpu.roll(uk, cols - 1, 1))
            vn = jnp.where(row == rows - 1, vnorth[m, pl.ds(k, 1), :], pltpu.roll(vk, rows - 1, 0))
            part = pk - horiz_ratio * s[k] * ((ue - uk) + (vn - vk))
            if not last_sub:
                u[m, k] = uk
                v[m, k] = vk
            p[m, k] = part
            return uk, vk, part

        def one(i, c):
            k = i + 1
            part_below, value, usum, vsum = c
            uk, vk, part = level(k)
            rhs = w[m, i] - vert_ratio * (part - part_below)
            value = (rhs + (vert_ratio * vert_ratio) * s[i] * value) * inv[k]
            w[m, i] = value
            if last_sub:
                usum = usum + thick[k] * uk
                vsum = vsum + thick[k] * vk
            return part, value, usum, vsum

        uk, vk, part = level(0)
        if last_sub:
            sums = (thick[0] * uk, thick[0] * vk)
            c = unrolled(levels - 1, one, (part, zero) + sums)
            return c[2], c[3]

        def two(i, c):
            return one(i, c + (None, None))[:2]

        unrolled(levels - 1, two, (part, zero))
        return None

    def backward(sub, m):
        last_sub = sub == SUBSTEPS - 1

        def finish(k, pk, c):
            if last_sub:
                return (c[0] + thick[k] * pk,)
            p[m, k] = pk
            rsend[sub + 1, m, 0, pl.ds(k, 1), :] = pk[rows - 1 : rows, :]
            rsend[sub + 1, m, 1, pl.ds(k, 1), :] = pk[0:1, :]
            return pack_last(k, pk, c[0]), pack_first(k, pk, c[1])

        def one(i, c):
            k = levels - 1 - i
            above = c[0]
            here = w[m, k - 1] + g[k] * above
            if not last_sub:
                w[m, k - 1] = here
            pk = p[m, k] - vert_ratio * s[k] * (above - here)
            return (here,) + finish(k, pk, c[1:])

        c = unrolled(levels - 1, one, (zero,) * (2 if last_sub else 3))
        pk = p[m, 0] - vert_ratio * s[0] * c[0]
        c = finish(0, pk, c[1:])
        if last_sub:
            return c[0]
        csend[sub + 1, m, 0] = c[0]
        csend[sub + 1, m, 1] = c[1]
        return None

    sent = []

    def send_halos(sub, m):
        for copy in halo_copies(sub, m):
            copy.start()
            sent.append(copy)

    for m in range(own):
        for name in "puv":
            loads[name, m].wait()
        pack_inputs(m)
        if m == 0:
            pl.semaphore_wait(barrier, tiles - 1 + n_mem - 1)
        send_halos(0, m)
        if m == 0:
            loads["s"].wait()
            pivots()

    for sub in range(SUBSTEPS):
        for m in range(own):
            if sub == 0:
                loads["w", m].wait()
            for copy in halo_copies(sub, m):
                copy.wait_recv()
            sums = forward(sub, m)
            mass = backward(sub, m)
            if sub < SUBSTEPS - 1:
                send_halos(sub + 1, m)
                continue
            for f, total in enumerate((mass,) + sums):
                for q in range(n_mem):
                    integ[m, q, f] = total[q * quarter : (q + 1) * quarter]
            for i in range(1, n_mem):
                other, where = mem_id(i)
                copy = remote(
                    integ.at[m, other], gath.at[mem, m], ms_sem.at[m, other], mr_sem.at[m, mem], where)
                copy.start()
                sent.append(copy)

    fields = [[integ[m, mem, f] for f in range(3)] for m in range(own)]
    for m in range(own):
        for i in range(1, n_mem):
            other, where = mem_id(i)
            remote(integ.at[m, other], gath.at[other, m], ms_sem.at[m, other], mr_sem.at[m, other], where).wait_recv()
            fields.append([gath[other, m, f] for f in range(3)])
    members = len(fields)
    for f in range(3):
        total = fields[0][f]
        for one in fields[1:]:
            total = total + one[f]
        mean = total / members
        second = (fields[0][f] - mean) ** 2
        for one in fields[1:]:
            second = second + (one[f] - mean) ** 2
        everyone[me, f] = mean
        everyone[me, 3 + f] = second / (members - 1)

    for i in range(1, tiles):
        other, where = tile_id(i)
        copy = remote(everyone.at[me], everyone.at[me], as_sem.at[i], ar_sem.at[me], where)
        copy.start()
        sent.append(copy)
    mine = jnp.int32(0)
    for t in range(tiles):
        mine = jnp.where(owner[t] == me, t, mine)
    for i in range(1, tiles):
        other, where = tile_id(i)
        remote(everyone.at[me], everyone.at[other], as_sem.at[i], ar_sem.at[other], where).wait_recv()
    out[0, 0] = everyone[mine]
    for copy in sent:
        copy.wait_send()


def solution(mesh):
    n_mem, n_ty, n_tx = (mesh.shape[a] for a in ("mem", "ty", "tx"))
    tiles = n_ty * n_tx

    def local(pressure, east_wind, north_wind, vertical_wind, sound_squared, thickness, owner_map):
        own, levels, rows, cols = pressure.shape
        quarter = rows // n_mem
        f32 = jnp.float32
        dma = pltpu.SemaphoreType.DMA
        anywhere = pl.BlockSpec(memory_space=pl.ANY)
        scalars = pl.BlockSpec(memory_space=pltpu.SMEM)
        return pl.pallas_call(
            functools.partial(kernel, (n_mem, n_ty, n_tx)),
            name="acoustic",
            out_shape=jax.ShapeDtypeStruct((1, 1, 6, quarter, cols), f32),
            in_specs=[anywhere] * 5 + [scalars] * 2,
            out_specs=pl.BlockSpec(memory_space=pltpu.VMEM),
            scratch_shapes=[
                pltpu.VMEM((own, levels, rows, cols), f32),
                pltpu.VMEM((own, levels, rows, cols), f32),
                pltpu.VMEM((own, levels, rows, cols), f32),
                pltpu.VMEM((own, levels - 1, rows, cols), f32),
                pltpu.VMEM((levels, rows, cols), f32),
                pltpu.VMEM((levels, rows, cols), f32),
                pltpu.VMEM((levels, rows, cols), f32),
                pltpu.VMEM((SUBSTEPS, own, 3, rows, cols), f32),
                pltpu.VMEM((SUBSTEPS, own, 3, rows, cols), f32),
                pltpu.VMEM((SUBSTEPS, own, 3, levels, cols), f32),
                pltpu.VMEM((SUBSTEPS, own, 3, levels, cols), f32),
                pltpu.VMEM((own, rows, cols), f32),
                pltpu.VMEM((own, levels, cols), f32),
                pltpu.VMEM((own, n_mem, 3, quarter, cols), f32),
                pltpu.VMEM((n_mem, own, 3, quarter, cols), f32),
                pltpu.VMEM((tiles, 6, quarter, cols), f32),
                dma((4 * own + 1,)),
                dma((SUBSTEPS, own, 3)),
                dma((SUBSTEPS, own, 3)),
                dma((SUBSTEPS, own, 3)),
                dma((SUBSTEPS, own, 3)),
                dma((own, n_mem)),
                dma((own, n_mem)),
                dma((tiles,)),
                dma((tiles,)),
            ],
            compiler_params=pltpu.CompilerParams(collective_id=0, has_side_effects=True),
        )(pressure, east_wind, north_wind, vertical_wind, sound_squared, thickness, owner_map)

    field = P("mem", None, "ty", "tx")
    return jax.shard_map(
        local,
        mesh=mesh,
        in_specs=(field, field, field, field, P(None, "ty", "tx"), P(), P()),
        out_specs=P("ty", "tx", None, "mem", None),
        check_vma=False,
    )
```

time: 222 us -> 33.3 us (0.15); the launches traced: 219 us -> 33.1 us
  other arithmetic: 69 us -> 0 us
  local copies, waits for them, and re-layouts: 68.2 us -> 1.35 us
  blocking collectives: 55 us -> 0 us
  Pallas kernels: 0 us -> 31.7 us
  starting transfers between devices: 10.6 us -> 0 us
  matrix products: 8.58 us -> 0 us
  waiting for transfers between devices: 3.6 us -> 0 us
  between operations: 3.49 us -> 0.01 us
    unnamed x528 -> x1, local copies, waits for them, and re-layouts: 38.2 us -> 1.35 us
    all_gather x1 -> x0, blocking collectives: 33.3 us -> none  [local(): lax.all_gather(stats[None], ('ty', 'tx'), axis=0, tiled=True)]
    pallas_call x0 -> x1, Pallas kernels: none -> 31.7 us  [local(): pl.pallas_call(functools.partial(kernel, (n_mem, n_ty, n_tx)), name='acou...]
    mul x43 -> x0, other arithmetic: 28.9 us -> none  [the longest x42 26.3 us: column_solve(): solved.insert(0, values[position] - factors[position] * solved[0])]
    psum x2 -> x0, blocking collectives: 21.7 us -> none  [local(): first_sum, second_sum = lax.psum((first_local, second_local), 'mem')]
    sub x6 -> x0, other arithmetic: 20.3 us -> none  [the longest x2 9.56 us: substep_run(): east_wind = east_wind - horiz_ratio * (pressure - pressure_west)]
    slice x13 -> x0, local copies, waits for them, and re-layouts: 18.3 us -> none  [the longest x3 4.18 us: substep_run(): western = shifted(pressure[..., -1:], 'tx', 1)]
    ppermute x4 -> x0, local copies, waits for them, and re-layouts: 11.6 us -> none  [shifted(): return lax.ppermute(block, axis, route)]
  transfers between devices with their start and end apart: 8 -> 0, of which waited for: 1 -> 0; matrix products, arithmetic and copies ran while one was open for 28% -> 0% of each run, Pallas kernels for 0% -> 0%
where the time goes in v1:
time: 33.3 us; the launch traced here: 33.1 us
  Pallas kernels  31.7 us (95%)
  local copies, waits for them, and re-layouts  1.35 us (4%)
    pallas_call x1, Pallas kernels, local(): pl.pallas_call(functools.partial(kernel, (n_mem, n_ty, n_tx)), name='acou...  31.7 us
    unnamed x1, local copies, waits for them, and re-layouts  1.35 us

profile of v1, /device:TPU:0, one launch (start us, length us, event | category | flops | bytes accessed | tf_op | source)
XLA Modules:
  0.0 33.1 jit_solution(10345000903072345179)
XLA Ops:
  0.0 31.7 %acoustic.1 = f32[1,1,6,8,128]{4,3,2,1,0:T(8,128)} custom-call(f32[2,50,32,128]{3,2,1,0:T(8,128)} %p_hbm.1, f32[2,50,32,128]{3,2,1,0:T(8,128)} %u_hbm.1, f32[2,50,32,128]{3,2,1,0:T(8,128)} %v_hbm.1, f32[2,49,32,128]{3,2,1,0:T(8,128)} %w_hbm.1, f32[50,32,128]{2,1,0:T(8,128)} %s_hbm.1, f32[50]{0:T(128)} %thick.1, s32[8]{0:T(128)} %owner.1), custom_call_target="tpu_custom_call" | custom-call | tf_op jit(solution)/shard_map/acoustic/pallas_call | solution.py:290
  31.7 1.3 %copy.9 = f32[1,1,6,8,128]{4,3,2,1,0:T(8,128)} copy(f32[1,1,6,8,128]{4,3,2,1,0:T(8,128)} %acoustic.1) | data formatting | bytes 49152

commit v2 on v1

--- a/solution.py
+++ b/solution.py
@@ -29,7 +29,7 @@
     sizes,
     p_hbm, u_hbm, v_hbm, w_hbm, s_hbm, thick, owner,
     out,
-    p, u, v, w, s, inv, g,
+    p, u, v, w, s, inv, g, lam, sig, alpha, edge_cols, edge_rows,
     csend, crecv, rsend, rrecv, ueast, vnorth,
     integ, gath, everyone,
     load_sem, cs_sem, cr_sem, rs_sem, rr_sem, ms_sem, mr_sem, as_sem, ar_sem,
@@ -45,18 +45,18 @@
     lane = lax.broadcasted_iota(jnp.int32, (rows, cols), 1)
     row = lax.broadcasted_iota(jnp.int32, (rows, cols), 0)
     zero = jnp.zeros((rows, cols), jnp.float32)
+    lane8 = lax.broadcasted_iota(jnp.int32, (8, cols), 1)
+    zero8 = jnp.zeros((8, cols), jnp.float32)
 
     def load(src, dst, sem):
         copy = pltpu.make_async_copy(src, dst, load_sem.at[sem])
         copy.start()
         return copy
 
-    loads = {}
+    loads = {"s": load(s_hbm, s, 4 * own)}
     for m in range(own):
         for i, (name, src, dst) in enumerate((("p", p_hbm, p), ("u", u_hbm, u), ("v", v_hbm, v))):
             loads[name, m] = load(src.at[m], dst.at[m], 4 * m + i)
-        if m == 0:
-            loads["s"] = load(s_hbm, s, 4 * own)
     for m in range(own):
         loads["w", m] = load(w_hbm.at[m], w.at[m], 4 * m + 3)
 
@@ -118,90 +118,115 @@
     def pivots():
         def one(i, c):
             k = i + 1
-            below, gprev = c
-            b = (vert_ratio * vert_ratio) * s[k]
+            below, gprev, mass_below, value = c
+            sk = s[k]
+            b = (vert_ratio * vert_ratio) * sk
+            mass = thick[k] * sk
             r = 1.0 / (1.0 + b + below - below * gprev)
+            gk = b * r
+            value = (vert_ratio * (mass - mass_below) + below * value) * r
             inv[k] = r
-            gk = b * r
             g[k] = gk
-            return b, gk
-
-        unrolled(levels - 1, one, ((vert_ratio * vert_ratio) * s[0], zero))
-
-    def forward(sub, m):
-        last_sub = sub == SUBSTEPS - 1
-        before = crecv[0, m, 2] if sub == 0 else ueast[m]
-        ueast[m] = before - horiz_ratio * (crecv[sub, m, 1] - csend[sub, m, 0])
-        before = rrecv[0, m, 2] if sub == 0 else vnorth[m]
-        vnorth[m] = before - horiz_ratio * (rrecv[sub, m, 1] - rsend[sub, m, 0])
-
-        def level(k):
+            lam[k] = value
+            return b, gk, mass, value
+
+        unrolled(levels - 1, one, ((vert_ratio * vert_ratio) * s[0], zero, thick[0] * s[0], zero))
+
+        def weights(k, here, above, first, last, mass):
+            mu = thick[k] - vert_ratio * (here - above)
+            sk = (horiz_ratio * horiz_ratio) * mu * s[k]
+            sig[k] = sk
+            alpha[k] = mu - 4.0 * sk
+            edge_rows[0, pl.ds(k, 1), :] = sk[0:1, :]
+            edge_rows[1, pl.ds(k, 1), :] = sk[rows - 1 : rows, :]
+            edge_rows[2, pl.ds(k, 1), :] = jnp.zeros((1, cols), jnp.float32) + thick[k]
+            mass = jnp.where(lane8 == cols - 1 - k, thick[k], mass)
+            return pack_first(k, sk, first), pack_last(k, sk, last), mass
+
+        def two(i, c):
+            k = levels - 1 - i
+            here = lam[k] + g[k] * c[0]
+            lam[k] = here
+            return (here,) + weights(k, here, *c)
+
+        c = unrolled(levels - 1, two, (zero, zero, zero, zero8))
+        first, last, mass = weights(0, zero, *c)
+        edge_cols[0] = first
+        edge_cols[1] = last
+        edge_cols[2] = jnp.concatenate([mass] * (rows // 8), axis=0)
+
+    def forward(m):
+        ueast[m] = crecv[0, m, 2] - horiz_ratio * (crecv[0, m, 1] - csend[0, m, 0])
+        vnorth[m] = rrecv[0, m, 2] - horiz_ratio * (rrecv[0, m, 1] - rsend[0, m, 0])
+
+        def level(k, usum, vsum, dsum):
             pk = p[m, k]
-            pw = jnp.where(lane == 0, pltpu.roll(crecv[sub, m, 0], k + 1, 1), pltpu.roll(pk, 1, 1))
-            ps = jnp.where(row == 0, rrecv[sub, m, 0, pl.ds(k, 1), :], pltpu.roll(pk, 1, 0))
+            pw = jnp.where(lane == 0, pltpu.roll(crecv[0, m, 0], k + 1, 1), pltpu.roll(pk, 1, 1))
+            ps = jnp.where(row == 0, rrecv[0, m, 0, pl.ds(k, 1), :], pltpu.roll(pk, 1, 0))
             uk = u[m, k] - horiz_ratio * (pk - pw)
             vk = v[m, k] - horiz_ratio * (pk - ps)
             ue = jnp.where(lane == cols - 1, pltpu.roll(ueast[m], k, 1), pltpu.roll(uk, cols - 1, 1))
             vn = jnp.where(row == rows - 1, vnorth[m, pl.ds(k, 1), :], pltpu.roll(vk, rows - 1, 0))
-            part = pk - horiz_ratio * s[k] * ((ue - uk) + (vn - vk))
-            if not last_sub:
-                u[m, k] = uk
-                v[m, k] = vk
+            div = (ue - uk) + (vn - vk)
+            part = pk - horiz_ratio * s[k] * div
             p[m, k] = part
-            return uk, vk, part
+            return part, usum + thick[k] * uk, vsum + thick[k] * vk, dsum + sig[k] * div
 
         def one(i, c):
             k = i + 1
-            part_below, value, usum, vsum = c
-            uk, vk, part = level(k)
+            part_below, value = c[:2]
+            part, *sums = level(k, *c[2:])
             rhs = w[m, i] - vert_ratio * (part - part_below)
             value = (rhs + (vert_ratio * vert_ratio) * s[i] * value) * inv[k]
             w[m, i] = value
-            if last_sub:
-                usum = usum + thick[k] * uk
-                vsum = vsum + thick[k] * vk
-            return part, value, usum, vsum
-
-        uk, vk, part = level(0)
-        if last_sub:
-            sums = (thick[0] * uk, thick[0] * vk)
-            c = unrolled(levels - 1, one, (part, zero) + sums)
-            return c[2], c[3]
-
-        def two(i, c):
-            return one(i, c + (None, None))[:2]
-
-        unrolled(levels - 1, two, (part, zero))
-        return None
-
-    def backward(sub, m):
-        last_sub = sub == SUBSTEPS - 1
-
+            return (part, value, *sums)
+
+        part, *sums = level(0, zero, zero, zero)
+        return unrolled(levels - 1, one, (part, zero, *sums))[2:]
+
+    def backward(m):
         def finish(k, pk, c):
-            if last_sub:
-                return (c[0] + thick[k] * pk,)
-            p[m, k] = pk
-            rsend[sub + 1, m, 0, pl.ds(k, 1), :] = pk[rows - 1 : rows, :]
-            rsend[sub + 1, m, 1, pl.ds(k, 1), :] = pk[0:1, :]
-            return pack_last(k, pk, c[0]), pack_first(k, pk, c[1])
+            last, first, mass, total = c
+            rsend[1, m, 0, pl.ds(k, 1), :] = pk[rows - 1 : rows, :]
+            rsend[1, m, 1, pl.ds(k, 1), :] = pk[0:1, :]
+            around = (pltpu.roll(pk, 1, 1) + pltpu.roll(pk, cols - 1, 1)) + (
+                pltpu.roll(pk, 1, 0) + pltpu.roll(pk, rows - 1, 0))
+            total = total + (alpha[k] * pk + sig[k] * around)
+            return pack_last(k, pk, last), pack_first(k, pk, first), mass + thick[k] * pk, total
 
         def one(i, c):
             k = levels - 1 - i
             above = c[0]
             here = w[m, k - 1] + g[k] * above
-            if not last_sub:
-                w[m, k - 1] = here
             pk = p[m, k] - vert_ratio * s[k] * (above - here)
-            return (here,) + finish(k, pk, c[1:])
-
-        c = unrolled(levels - 1, one, (zero,) * (2 if last_sub else 3))
+            last, first, mass, total = finish(k, pk, c[1:])
+            return here, last, first, mass, total + lam[k] * here
+
+        c = unrolled(levels - 1, one, (zero,) * 5)
         pk = p[m, 0] - vert_ratio * s[0] * c[0]
-        c = finish(0, pk, c[1:])
-        if last_sub:
-            return c[0]
-        csend[sub + 1, m, 0] = c[0]
-        csend[sub + 1, m, 1] = c[1]
-        return None
+        last, first, mass, total = finish(0, pk, c[1:])
+        csend[1, m, 0] = last
+        csend[1, m, 1] = first
+        return mass, total
+
+    def integrals(m, usum, vsum, dsum, mass, total):
+        across = lambda x: jnp.sum(x, axis=1, keepdims=True)
+        along = lambda x: jnp.sum(x, axis=0, keepdims=True)
+        pw, ps = crecv[1, m, 0], rrecv[1, m, 0]
+        total = total - dsum / horiz_ratio
+        total = total + jnp.where(lane == 0, across(edge_cols[0] * (pw - csend[1, m, 0])), 0.0)
+        total = total + jnp.where(
+            lane == cols - 1, across(edge_cols[1] * (crecv[1, m, 1] - csend[1, m, 1])), 0.0)
+        total = total + jnp.where(row == 0, along(edge_rows[0] * (ps - rsend[1, m, 0])), 0.0)
+        total = total + jnp.where(
+            row == rows - 1, along(edge_rows[1] * (rrecv[1, m, 1] - rsend[1, m, 1])), 0.0)
+        mass_west = jnp.where(lane == 0, across(edge_cols[2] * pw), pltpu.roll(mass, 1, 1))
+        mass_south = jnp.where(row == 0, along(edge_rows[2] * ps), pltpu.roll(mass, 1, 0))
+        return (
+            total,
+            usum - horiz_ratio * (mass - mass_west),
+            vsum - horiz_ratio * (mass - mass_south),
+        )
 
     sent = []
 
@@ -210,6 +235,8 @@
             copy.start()
             sent.append(copy)
 
+    loads["s"].wait()
+    pivots()
     for m in range(own):
         for name in "puv":
             loads[name, m].wait()
@@ -217,30 +244,26 @@
         if m == 0:
             pl.semaphore_wait(barrier, tiles - 1 + n_mem - 1)
         send_halos(0, m)
-        if m == 0:
-            loads["s"].wait()
-            pivots()
-
-    for sub in range(SUBSTEPS):
-        for m in range(own):
-            if sub == 0:
-                loads["w", m].wait()
-            for copy in halo_copies(sub, m):
-                copy.wait_recv()
-            sums = forward(sub, m)
-            mass = backward(sub, m)
-            if sub < SUBSTEPS - 1:
-                send_halos(sub + 1, m)
-                continue
-            for f, total in enumerate((mass,) + sums):
-                for q in range(n_mem):
-                    integ[m, q, f] = total[q * quarter : (q + 1) * quarter]
-            for i in range(1, n_mem):
-                other, where = mem_id(i)
-                copy = remote(
-                    integ.at[m, other], gath.at[mem, m], ms_sem.at[m, other], mr_sem.at[m, mem], where)
-                copy.start()
-                sent.append(copy)
+
+    sums = []
+    for m in range(own):
+        loads["w", m].wait()
+        for copy in halo_copies(0, m):
+            copy.wait_recv()
+        sums.append((*forward(m), *backward(m)))
+        send_halos(1, m)
+    for m in range(own):
+        for copy in halo_copies(1, m):
+            copy.wait_recv()
+        for f, total in enumerate(integrals(m, *sums[m])):
+            for q in range(n_mem):
+                integ[m, q, f] = total[q * quarter : (q + 1) * quarter]
+        for i in range(1, n_mem):
+            other, where = mem_id(i)
+            copy = remote(
+                integ.at[m, other], gath.at[mem, m], ms_sem.at[m, other], mr_sem.at[m, mem], where)
+            copy.start()
+            sent.append(copy)
 
     fields = [[integ[m, mem, f] for f in range(3)] for m in range(own)]
     for m in range(own):
@@ -298,9 +321,9 @@
                 pltpu.VMEM((own, levels, rows, cols), f32),
                 pltpu.VMEM((own, levels, rows, cols), f32),
                 pltpu.VMEM((own, levels - 1, rows, cols), f32),
-                pltpu.VMEM((levels, rows, cols), f32),
-                pltpu.VMEM((levels, rows, cols), f32),
-                pltpu.VMEM((levels, rows, cols), f32),
+                *[pltpu.VMEM((levels, rows, cols), f32)] * 6,
+                pltpu.VMEM((3, rows, cols), f32),
+                pltpu.VMEM((3, levels, cols), f32),
                 pltpu.VMEM((SUBSTEPS, own, 3, rows, cols), f32),
                 pltpu.VMEM((SUBSTEPS, own, 3, rows, cols), f32),
                 pltpu.VMEM((SUBSTEPS, own, 3, levels, cols), f32),

time: 33.3 us -> 33.9 us (1.018)
  Pallas kernels: 31.7 us -> 32.3 us
    pallas_call x1, Pallas kernels: 31.7 us -> 32.3 us  [local(): pl.pallas_call(functools.partial(kernel, (n_mem, n_ty, n_tx)), name='acou...]
where the time goes in v2:
time: 33.9 us; the launch traced here: 33.7 us
  Pallas kernels  32.3 us (95%)
  local copies, waits for them, and re-layouts  1.35 us (4%)
    pallas_call x1, Pallas kernels, local(): pl.pallas_call(functools.partial(kernel, (n_mem, n_ty, n_tx)), name='acou...  32.3 us
    unnamed x1, local copies, waits for them, and re-layouts  1.35 us

profile of v2, /device:TPU:0, one launch (start us, length us, event | category | flops | bytes accessed | tf_op | source)
XLA Modules:
  0.0 33.7 jit_solution(1950135398091121025)
XLA Ops:
  0.0 32.3 %acoustic.1 = f32[1,1,6,8,128]{4,3,2,1,0:T(8,128)} custom-call(f32[2,50,32,128]{3,2,1,0:T(8,128)} %p_hbm.1, f32[2,50,32,128]{3,2,1,0:T(8,128)} %u_hbm.1, f32[2,50,32,128]{3,2,1,0:T(8,128)} %v_hbm.1, f32[2,49,32,128]{3,2,1,0:T(8,128)} %w_hbm.1, f32[50,32,128]{2,1,0:T(8,128)} %s_hbm.1, f32[50]{0:T(128)} %thick.1, s32[8]{0:T(128)} %owner.1), custom_call_target="tpu_custom_call" | custom-call | tf_op jit(solution)/shard_map/acoustic/pallas_call | solution.py:313
  32.3 1.3 %copy.9 = f32[1,1,6,8,128]{4,3,2,1,0:T(8,128)} copy(f32[1,1,6,8,128]{4,3,2,1,0:T(8,128)} %acoustic.1) | data formatting | bytes 49152

commit v3 on v2

--- a/solution.py
+++ b/solution.py
@@ -62,9 +62,13 @@
 
     barrier = pltpu.get_barrier_semaphore()
 
+    far = lambda d: -(min(d[0], n_ty - d[0]) + min(d[1], n_tx - d[1]))
+    offsets = sorted([(a, b) for a in range(n_ty) for b in range(n_tx)], key=far)
+
     def tile_id(i):
-        other = lax.rem(me + i, tiles)
-        return other, {"ty": lax.div(other, n_tx), "tx": lax.rem(other, n_tx)}
+        a, b = offsets[i - 1]
+        other_ty, other_tx = lax.rem(ty + a, n_ty), lax.rem(tx + b, n_tx)
+        return other_ty * n_tx + other_tx, {"ty": other_ty, "tx": other_tx}
 
     def mem_id(i):
         other = lax.rem(mem + i, n_mem)
@@ -81,9 +85,9 @@
         )
 
     def halo_copies(sub, m):
-        kinds = ((0, east, north), (1, west, south), (2, west, south))
+        kinds = ((0, east, north), (1, west, south))
         copies = []
-        for kind, across, along in kinds if sub == 0 else kinds[:2]:
+        for kind, across, along in kinds:
             copies.append(remote(
                 rsend.at[sub, m, kind], rrecv.at[sub, m, kind],
                 rs_sem.at[sub, m, kind], rr_sem.at[sub, m, kind], along))
@@ -101,18 +105,16 @@
 
     def pack_inputs(m):
         def one(k, c):
-            last, first, ufirst = c
+            last, first = c
             pk = p[m, k]
-            first = pack_first(k, pk, first)
+            first = pack_first(k, u[m, k] - horiz_ratio * pk, first)
             last = jnp.where(lane == cols - 1 - k, pltpu.roll(pk, lax.rem(cols - k, cols), 1), last)
-            ufirst = pack_first(k, u[m, k], ufirst)
             rsend[0, m, 0, pl.ds(k, 1), :] = p[m, k, rows - 1 : rows, :]
-            rsend[0, m, 1, pl.ds(k, 1), :] = p[m, k, 0:1, :]
-            rsend[0, m, 2, pl.ds(k, 1), :] = v[m, k, 0:1, :]
-            return last, first, ufirst
-
-        packs = unrolled(levels, one, (zero, zero, zero), 5)
-        for kind in range(3):
+            rsend[0, m, 1, pl.ds(k, 1), :] = v[m, k, 0:1, :] - horiz_ratio * p[m, k, 0:1, :]
+            return last, first
+
+        packs = unrolled(levels, one, (zero, zero), 5)
+        for kind in range(2):
             csend[0, m, kind] = packs[kind]
 
     def pivots():
@@ -156,8 +158,8 @@
         edge_cols[2] = jnp.concatenate([mass] * (rows // 8), axis=0)
 
     def forward(m):
-        ueast[m] = crecv[0, m, 2] - horiz_ratio * (crecv[0, m, 1] - csend[0, m, 0])
-        vnorth[m] = rrecv[0, m, 2] - horiz_ratio * (rrecv[0, m, 1] - rsend[0, m, 0])
+        ueast[m] = crecv[0, m, 1] + horiz_ratio * csend[0, m, 0]
+        vnorth[m] = rrecv[0, m, 1] + horiz_ratio * rsend[0, m, 0]
 
         def level(k, usum, vsum, dsum):
             pk = p[m, k]
@@ -185,29 +187,37 @@
         return unrolled(levels - 1, one, (part, zero, *sums))[2:]
 
     def backward(m):
-        def finish(k, pk, c):
-            last, first, mass, total = c
+        def finish(k, pk, last, first):
+            p[m, k] = pk
             rsend[1, m, 0, pl.ds(k, 1), :] = pk[rows - 1 : rows, :]
             rsend[1, m, 1, pl.ds(k, 1), :] = pk[0:1, :]
-            around = (pltpu.roll(pk, 1, 1) + pltpu.roll(pk, cols - 1, 1)) + (
-                pltpu.roll(pk, 1, 0) + pltpu.roll(pk, rows - 1, 0))
-            total = total + (alpha[k] * pk + sig[k] * around)
-            return pack_last(k, pk, last), pack_first(k, pk, first), mass + thick[k] * pk, total
+            return pack_last(k, pk, last), pack_first(k, pk, first)
 
         def one(i, c):
             k = levels - 1 - i
             above = c[0]
             here = w[m, k - 1] + g[k] * above
+            w[m, k - 1] = here
             pk = p[m, k] - vert_ratio * s[k] * (above - here)
-            last, first, mass, total = finish(k, pk, c[1:])
-            return here, last, first, mass, total + lam[k] * here
-
-        c = unrolled(levels - 1, one, (zero,) * 5)
-        pk = p[m, 0] - vert_ratio * s[0] * c[0]
-        last, first, mass, total = finish(0, pk, c[1:])
+            return (here,) + finish(k, pk, c[1], c[2])
+
+        c = unrolled(levels - 1, one, (zero,) * 3)
+        last, first = finish(0, p[m, 0] - vert_ratio * s[0] * c[0], c[1], c[2])
         csend[1, m, 0] = last
         csend[1, m, 1] = first
-        return mass, total
+
+    def weigh(m):
+        def level(k, mass, total):
+            pk = p[m, k]
+            around = (pltpu.roll(pk, 1, 1) + pltpu.roll(pk, cols - 1, 1)) + (
+                pltpu.roll(pk, 1, 0) + pltpu.roll(pk, rows - 1, 0))
+            return mass + thick[k] * pk, total + (alpha[k] * pk + sig[k] * around)
+
+        def one(i, c):
+            mass, total = level(i + 1, *c)
+            return mass, total + lam[i + 1] * w[m, i]
+
+        return unrolled(levels - 1, one, level(0, zero, zero))
 
     def integrals(m, usum, vsum, dsum, mass, total):
         across = lambda x: jnp.sum(x, axis=1, keepdims=True)
@@ -250,8 +260,10 @@
         loads["w", m].wait()
         for copy in halo_copies(0, m):
             copy.wait_recv()
-        sums.append((*forward(m), *backward(m)))
+        sums.append(forward(m))
+        backward(m)
         send_halos(1, m)
+    sums = [(*sums[m], *weigh(m)) for m in range(own)]
     for m in range(own):
         for copy in halo_copies(1, m):
             copy.wait_recv()
@@ -324,20 +336,20 @@
                 *[pltpu.VMEM((levels, rows, cols), f32)] * 6,
                 pltpu.VMEM((3, rows, cols), f32),
                 pltpu.VMEM((3, levels, cols), f32),
-                pltpu.VMEM((SUBSTEPS, own, 3, rows, cols), f32),
-                pltpu.VMEM((SUBSTEPS, own, 3, rows, cols), f32),
-                pltpu.VMEM((SUBSTEPS, own, 3, levels, cols), f32),
-                pltpu.VMEM((SUBSTEPS, own, 3, levels, cols), f32),
+                pltpu.VMEM((SUBSTEPS, own, 2, rows, cols), f32),
+                pltpu.VMEM((SUBSTEPS, own, 2, rows, cols), f32),
+                pltpu.VMEM((SUBSTEPS, own, 2, levels, cols), f32),
+                pltpu.VMEM((SUBSTEPS, own, 2, levels, cols), f32),
                 pltpu.VMEM((own, rows, cols), f32),
                 pltpu.VMEM((own, levels, cols), f32),
                 pltpu.VMEM((own, n_mem, 3, quarter, cols), f32),
                 pltpu.VMEM((n_mem, own, 3, quarter, cols), f32),
                 pltpu.VMEM((tiles, 6, quarter, cols), f32),
                 dma((4 * own + 1,)),
-                dma((SUBSTEPS, own, 3)),
-                dma((SUBSTEPS, own, 3)),
-                dma((SUBSTEPS, own, 3)),
-                dma((SUBSTEPS, own, 3)),
+                dma((SUBSTEPS, own, 2)),
+                dma((SUBSTEPS, own, 2)),
+                dma((SUBSTEPS, own, 2)),
+                dma((SUBSTEPS, own, 2)),
                 dma((own, n_mem)),
                 dma((own, n_mem)),
                 dma((tiles,)),

time: 33.9 us -> 32.6 us (0.962)
  Pallas kernels: 32.3 us -> 31.1 us
    pallas_call x1, Pallas kernels: 32.3 us -> 31.1 us  [local(): pl.pallas_call(functools.partial(kernel, (n_mem, n_ty, n_tx)), name='acou...]
where the time goes in v3:
time: 32.6 us; the launch traced here: 32.5 us
  Pallas kernels  31.1 us (95%)
  local copies, waits for them, and re-layouts  1.35 us (4%)
    pallas_call x1, Pallas kernels, local(): pl.pallas_call(functools.partial(kernel, (n_mem, n_ty, n_tx)), name='acou...  31.1 us
    unnamed x1, local copies, waits for them, and re-layouts  1.35 us

profile of v3, /device:TPU:0, one launch (start us, length us, event | category | flops | bytes accessed | tf_op | source)
XLA Modules:
  0.0 32.5 jit_solution(1795813856380337810)
XLA Ops:
  0.0 31.1 %acoustic.1 = f32[1,1,6,8,128]{4,3,2,1,0:T(8,128)} custom-call(f32[2,50,32,128]{3,2,1,0:T(8,128)} %p_hbm.1, f32[2,50,32,128]{3,2,1,0:T(8,128)} %u_hbm.1, f32[2,50,32,128]{3,2,1,0:T(8,128)} %v_hbm.1, f32[2,49,32,128]{3,2,1,0:T(8,128)} %w_hbm.1, f32[50,32,128]{2,1,0:T(8,128)} %s_hbm.1, f32[50]{0:T(128)} %thick.1, s32[8]{0:T(128)} %owner.1), custom_call_target="tpu_custom_call" | custom-call | tf_op jit(solution)/shard_map/acoustic/pallas_call | solution.py:325
  31.1 1.3 %copy.9 = f32[1,1,6,8,128]{4,3,2,1,0:T(8,128)} copy(f32[1,1,6,8,128]{4,3,2,1,0:T(8,128)} %acoustic.1) | data formatting | bytes 49152

commit v4 on v3

--- a/solution.py
+++ b/solution.py
@@ -105,17 +105,19 @@
 
     def pack_inputs(m):
         def one(k, c):
-            last, first = c
+            last, first, usum, vsum, mass = c
             pk = p[m, k]
             first = pack_first(k, u[m, k] - horiz_ratio * pk, first)
             last = jnp.where(lane == cols - 1 - k, pltpu.roll(pk, lax.rem(cols - k, cols), 1), last)
             rsend[0, m, 0, pl.ds(k, 1), :] = p[m, k, rows - 1 : rows, :]
             rsend[0, m, 1, pl.ds(k, 1), :] = v[m, k, 0:1, :] - horiz_ratio * p[m, k, 0:1, :]
-            return last, first
-
-        packs = unrolled(levels, one, (zero, zero), 5)
+            uk, vk, pk = thick[k] * u[m, k], thick[k] * v[m, k], thick[k] * pk
+            return last, first, usum + uk, vsum + vk, mass + pk
+
+        packs = unrolled(levels, one, (zero,) * 5, 5)
         for kind in range(2):
             csend[0, m, kind] = packs[kind]
+        return packs[2:]
 
     def pivots():
         def one(i, c):
@@ -161,7 +163,7 @@
         ueast[m] = crecv[0, m, 1] + horiz_ratio * csend[0, m, 0]
         vnorth[m] = rrecv[0, m, 1] + horiz_ratio * rsend[0, m, 0]
 
-        def level(k, usum, vsum, dsum):
+        def level(k, dsum):
             pk = p[m, k]
             pw = jnp.where(lane == 0, pltpu.roll(crecv[0, m, 0], k + 1, 1), pltpu.roll(pk, 1, 1))
             ps = jnp.where(row == 0, rrecv[0, m, 0, pl.ds(k, 1), :], pltpu.roll(pk, 1, 0))
@@ -172,19 +174,19 @@
             div = (ue - uk) + (vn - vk)
             part = pk - horiz_ratio * s[k] * div
             p[m, k] = part
-            return part, usum + thick[k] * uk, vsum + thick[k] * vk, dsum + sig[k] * div
+            return part, dsum + sig[k] * div
 
         def one(i, c):
             k = i + 1
             part_below, value = c[:2]
-            part, *sums = level(k, *c[2:])
+            part, dsum = level(k, c[2])
             rhs = w[m, i] - vert_ratio * (part - part_below)
             value = (rhs + (vert_ratio * vert_ratio) * s[i] * value) * inv[k]
             w[m, i] = value
-            return (part, value, *sums)
-
-        part, *sums = level(0, zero, zero, zero)
-        return unrolled(levels - 1, one, (part, zero, *sums))[2:]
+            return part, value, dsum
+
+        part, dsum = level(0, zero)
+        return unrolled(levels - 1, one, (part, zero, dsum))[2]
 
     def backward(m):
         def finish(k, pk, last, first):
@@ -219,7 +221,7 @@
 
         return unrolled(levels - 1, one, level(0, zero, zero))
 
-    def integrals(m, usum, vsum, dsum, mass, total):
+    def integrals(m, usum, vsum, mass_before, dsum, mass, total):
         across = lambda x: jnp.sum(x, axis=1, keepdims=True)
         along = lambda x: jnp.sum(x, axis=0, keepdims=True)
         pw, ps = crecv[1, m, 0], rrecv[1, m, 0]
@@ -230,6 +232,7 @@
         total = total + jnp.where(row == 0, along(edge_rows[0] * (ps - rsend[1, m, 0])), 0.0)
         total = total + jnp.where(
             row == rows - 1, along(edge_rows[1] * (rrecv[1, m, 1] - rsend[1, m, 1])), 0.0)
+        mass, pw, ps = mass_before + mass, crecv[0, m, 0] + pw, rrecv[0, m, 0] + ps
         mass_west = jnp.where(lane == 0, across(edge_cols[2] * pw), pltpu.roll(mass, 1, 1))
         mass_south = jnp.where(row == 0, along(edge_rows[2] * ps), pltpu.roll(mass, 1, 0))
         return (
@@ -247,10 +250,11 @@
 
     loads["s"].wait()
     pivots()
+    raw = []
     for m in range(own):
         for name in "puv":
             loads[name, m].wait()
-        pack_inputs(m)
+        raw.append(pack_inputs(m))
         if m == 0:
             pl.semaphore_wait(barrier, tiles - 1 + n_mem - 1)
         send_halos(0, m)
@@ -260,7 +264,7 @@
         loads["w", m].wait()
         for copy in halo_copies(0, m):
             copy.wait_recv()
-        sums.append(forward(m))
+        sums.append((*raw[m], forward(m)))
         backward(m)
         send_halos(1, m)
     sums = [(*sums[m], *weigh(m)) for m in range(own)]

time: 32.6 us -> 32.7 us (level)
  no operation moved by 1% of the time
where the time goes in v4:
time: 32.7 us; the launch traced here: 32.5 us
  Pallas kernels  31.1 us (95%)
  local copies, waits for them, and re-layouts  1.35 us (4%)
    pallas_call x1, Pallas kernels, local(): pl.pallas_call(functools.partial(kernel, (n_mem, n_ty, n_tx)), name='acou...  31.1 us
    unnamed x1, local copies, waits for them, and re-layouts  1.35 us

profile of v4, /device:TPU:0, one launch (start us, length us, event | category | flops | bytes accessed | tf_op | source)
XLA Modules:
  0.0 32.5 jit_solution(9805520383491114852)
XLA Ops:
  0.0 31.1 %acoustic.1 = f32[1,1,6,8,128]{4,3,2,1,0:T(8,128)} custom-call(f32[2,50,32,128]{3,2,1,0:T(8,128)} %p_hbm.1, f32[2,50,32,128]{3,2,1,0:T(8,128)} %u_hbm.1, f32[2,50,32,128]{3,2,1,0:T(8,128)} %v_hbm.1, f32[2,49,32,128]{3,2,1,0:T(8,128)} %w_hbm.1, f32[50,32,128]{2,1,0:T(8,128)} %s_hbm.1, f32[50]{0:T(128)} %thick.1, s32[8]{0:T(128)} %owner.1), custom_call_target="tpu_custom_call" | custom-call | tf_op jit(solution)/shard_map/acoustic/pallas_call | solution.py:329
  31.1 1.3 %copy.9 = f32[1,1,6,8,128]{4,3,2,1,0:T(8,128)} copy(f32[1,1,6,8,128]{4,3,2,1,0:T(8,128)} %acoustic.1) | data formatting | bytes 49152
